TPU v7x, 32 devices: a whole 2x2x4 slice. The times are simulated.
32 devices in a mesh: dp: 16 (over z, y, x), mp: 2 (over core).
Axes of the slice: x: 2, y: 2, z: 4, core: 2. Of those that a mesh axis runs over, the one named last changes fastest.
Arguments:
- clean_latent: float32 [16, 4096], P('dp'), may hold values from -6 to 6
- noise_draw: float32 [16, 4096], P('dp'), may hold values from -6 to 6
- timestep: int32 [16], P('dp'), may hold values from 1 to 8
- bucket: int32 [16], P('dp'), may hold values from 0 to 7
- bucket_weights: float32 [8], replicated, may hold values from 0.25 to 4
- teacher_embed: float32 [16, 2048], replicated, may hold values from -1.5 to 1.5
- teacher_final: float32 [16, 2048], replicated, may hold values from -0.125 to 0.125
- teacher_mod: float32 [16, 3, 2048], replicated, may hold values from -3 to 3
- teacher_qkv: bfloat16 [2048, 3, 1024], P(None, None, 'mp'), may hold values from -1 to 1
- teacher_out: bfloat16 [2048, 1024], P(None, 'mp'), may hold values from -0.1875 to 0.1875
- student_embed: float32 [16, 2048], replicated, may hold values from -1.5 to 1.5
- student_final: float32 [16, 2048], replicated, may hold values from -0.125 to 0.125
- student_mod: float32 [8, 3, 2048], replicated, may hold values from -3 to 3
- student_qkv: bfloat16 [2048, 3, 1024], P('dp', None, 'mp'), may hold values from -1 to 1
- student_out: bfloat16 [2048, 1024], P('dp', 'mp'), may hold values from -0.1875 to 0.1875
- moment_qkv: float32 [2048, 3, 1024], P('dp', None, 'mp'), may hold values from -2 to 2
- second_qkv: float32 [2048, 3, 1024], P('dp', None, 'mp'), may hold values from 0.05 to 0.5
- moment_out: float32 [2048, 1024], P('dp', 'mp'), may hold values from -2 to 2
- second_out: float32 [2048, 1024], P('dp', 'mp'), may hold values from 0.05 to 0.5
Outputs:
- new_moment_qkv: float32 [2048, 3, 1024], P('dp', None, 'mp')
- new_second_qkv: float32 [2048, 3, 1024], P('dp', None, 'mp')
- update_qkv: float32 [2048, 3, 1024], P('dp', None, 'mp')
- new_moment_out: float32 [2048, 1024], P('dp', 'mp')
- new_second_out: float32 [2048, 1024], P('dp', 'mp')
- update_out: float32 [2048, 1024], P('dp', 'mp')
- loss: float32 [], replicated
All inputs are finite; a program needn't handle non-finite values.
Results may differ from a plain program's by a relative error of at most 0.00035.
Values may be sent and summed in bfloat16 or wider, within the bound.
No kernel may reach another device: no remote copies, remote signals or barrier semaphores. Data moves between devices by JAX's collectives and lax.ppermute only.
A program may use at most 128 MiB of HBM per device.

v0:
```python
import math
import jax
import jax.numpy as jnp
from jax import lax
from jax.sharding import PartitionSpec as P

D = 2048
HS = 64
INNER = 1024
PATCH_CH = 16
SEQ = 256
LATENT = 4096
K = 8
TGRID = 16
NBUCKET = 8
LN_EPS = 0.01
BETA_ONE = 0.9
BETA_TWO = 0.99
ADAM_EPS = 1e-08


def plan():
    grid = jnp.arange(TGRID + 1, dtype=jnp.float32)
    lamb = 6.0 - 12.0 * grid / TGRID
    return (jnp.sqrt(jax.nn.sigmoid(lamb)), jnp.sqrt(jax.nn.sigmoid(-lamb)))


def positions():
    index = jnp.arange(SEQ, dtype=jnp.float32)[:, None]
    half = D // 2
    freqs = jnp.exp(-math.log(10000.0) * jnp.arange(half, dtype=jnp.float32) / half)
    angles = index * freqs[None, :]
    return jnp.concatenate([jnp.sin(angles), jnp.cos(angles)], axis=1)


def normalize(values):
    center = values - jnp.mean(values, axis=-1, keepdims=True)
    inverse = lax.rsqrt(jnp.mean(center * center, axis=-1, keepdims=True) + LN_EPS)
    return (center * inverse, inverse)


def norm_back(upstream, normed, inverse):
    first_mean = jnp.mean(upstream, axis=-1, keepdims=True)
    second_mean = jnp.mean(upstream * normed, axis=-1, keepdims=True)
    return (upstream - first_mean - normed * second_mean) * inverse


def one_hot_rows(index, width):
    return (index[:, None] == jnp.arange(width, dtype=jnp.int32)[None, :]).astype(jnp.float32)


def per_device(
    clean_latent,
    noise_draw,
    timestep,
    bucket,
    bucket_weights,
    teacher_embed,
    teacher_final,
    teacher_mod,
    teacher_qkv,
    teacher_out,
    student_embed,
    student_final,
    student_mod,
    student_qkv,
    student_out,
    moment_qkv,
    second_qkv,
    moment_out,
    second_out,
):
    samples = clean_latent.shape[0]
    rows_all = samples * SEQ
    local_inner = teacher_out.shape[1]
    local_heads = local_inner // HS
    count = rows_all // lax.axis_size("mp")
    start = lax.axis_index("mp") * count

    def take(values):
        return lax.dynamic_slice_in_dim(values, start, count, 0)

    alphas, sigmas = plan()
    table = jnp.stack([alphas, sigmas], axis=1)

    def coefficients(tau):
        picked = jnp.dot(one_hot_rows(tau, TGRID + 1), table, precision=lax.Precision.HIGHEST)
        picked = jnp.repeat(picked, SEQ, axis=0)
        return (picked[:, 0:1], picked[:, 1:2])

    def modulation(mod_table, index, length):
        picked = jnp.dot(
            one_hot_rows(index, length),
            mod_table.reshape(length, 3 * D),
            precision=lax.Precision.HIGHEST,
        )
        return picked.reshape(samples, 3, D)

    def gate_rows(modrows):
        return take(jnp.repeat(modrows[:, 2], SEQ, axis=0))

    placed = positions()

    def front(latent, modrows, embed, w_qkv, w_out):
        hidden = (
            jnp.dot(latent, embed, precision=lax.Precision.HIGHEST).reshape(samples, SEQ, D)
            + placed[None]
        )
        normed, unused = normalize(hidden)
        shaped = (
            (normed * (1.0 + modrows[:, None, 1]) + modrows[:, None, 0])
            .astype(jnp.bfloat16)
            .reshape(rows_all, D)
        )
        hidden = hidden.reshape(rows_all, D)
        packed = jnp.dot(
            shaped, w_qkv.reshape(D, 3 * local_inner), preferred_element_type=jnp.float32
        )
        packed = packed.astype(jnp.bfloat16).reshape(samples, SEQ, 3, local_heads, HS)
        queries = packed[:, :, 0]
        keys_all = packed[:, :, 1]
        values = packed[:, :, 2]
        scores = jnp.einsum(
            "sqhd,skhd->shqk", queries, keys_all, preferred_element_type=jnp.float32
        ) / math.sqrt(HS)
        highest = jnp.max(scores, axis=-1, keepdims=True)
        expos = jnp.exp(scores - highest)
        weights = expos / jnp.sum(expos, axis=-1, keepdims=True)
        rounded = weights.astype(jnp.bfloat16)
        attended = jnp.einsum(
            "shqk,skhd->sqhd", rounded, values, preferred_element_type=jnp.float32
        )
        attended = attended.astype(jnp.bfloat16).reshape(rows_all, local_inner)
        projected = lax.dot_general(
            attended, w_out, (((1,), (1,)), ((), ())), preferred_element_type=jnp.float32
        )
        return (hidden, shaped, queries, keys_all, values, weights, rounded, attended, projected)

    def reduce_heads(projected):
        return lax.psum_scatter(projected, "mp", scatter_dimension=0, tiled=True)

    def tail(hidden, modrows, projected, final):
        mixed = take(hidden) + gate_rows(modrows) * reduce_heads(projected)
        normed, inverse = normalize(mixed)
        predicted = lax.dot_general(
            normed, final, (((1,), (1,)), ((), ())), precision=lax.Precision.HIGHEST
        )
        return (predicted, normed, inverse)

    def teacher_eps(latent, modrows):
        parts = front(latent, modrows, teacher_embed, teacher_qkv, teacher_out)
        return tail(parts[0], modrows, parts[8], teacher_final)[0]

    whole_qkv, whole_out = (
        lax.all_gather(student_qkv, "dp", axis=0, tiled=True),
        lax.all_gather(student_out, "dp", axis=0, tiled=True),
    )
    first = 2 * timestep
    middle = first - 1
    last = first - 2
    a_first, s_first = coefficients(first)
    a_middle, s_middle = coefficients(middle)
    a_last, s_last = coefficients(last)
    clean_rows = clean_latent.reshape(rows_all, PATCH_CH)
    noise_rows = noise_draw.reshape(rows_all, PATCH_CH)
    latent0 = a_first * clean_rows + s_first * noise_rows
    mine0 = take(latent0)
    af_mine, sf_mine = (take(a_first), take(s_first))
    am_mine, sm_mine = (take(a_middle), take(s_middle))
    al_mine, sl_mine = (take(a_last), take(s_last))
    eps_zero = teacher_eps(latent0, modulation(teacher_mod, first - 1, TGRID))
    next_mine = am_mine * (mine0 - sf_mine * eps_zero) / af_mine + sm_mine * eps_zero
    latent1 = lax.all_gather(next_mine, "mp", axis=0, tiled=True)
    eps_one = teacher_eps(latent1, modulation(teacher_mod, middle - 1, TGRID))
    latent2 = al_mine * (take(latent1) - sm_mine * eps_one) / am_mine + sl_mine * eps_one
    target = (mine0 - af_mine / al_mine * latent2) / (sf_mine - af_mine * sl_mine / al_mine)
    student_rows_mod = modulation(student_mod, timestep - 1, K)
    hidden, shaped, queries, keys_all, values, weights, rounded, attended, projected = front(
        latent0, student_rows_mod, student_embed, whole_qkv, whole_out
    )
    predicted, normed, inverse = tail(hidden, student_rows_mod, projected, student_final)
    sample_weight = jnp.dot(
        one_hot_rows(bucket, NBUCKET), bucket_weights, precision=lax.Precision.HIGHEST
    )
    row_weight = take(jnp.repeat(sample_weight, SEQ, axis=0)[:, None])
    error = predicted - target
    loss_part = jnp.sum(row_weight * error * error)
    d_pred = 2.0 * row_weight * error
    d_normed = jnp.dot(d_pred, student_final, precision=lax.Precision.HIGHEST)
    d_mixed = norm_back(d_normed, normed, inverse)
    d_proj_mine = (gate_rows(student_rows_mod) * d_mixed).astype(jnp.bfloat16)
    d_proj = lax.all_gather(d_proj_mine, "mp", axis=0, tiled=True)
    loss_sum = lax.psum(loss_part, ("dp", "mp"))
    d_attn = jnp.dot(d_proj, whole_out, preferred_element_type=jnp.float32).astype(jnp.bfloat16)
    d_attn = d_attn.reshape(samples, SEQ, local_heads, HS)
    d_prob = jnp.einsum("sqhd,skhd->shqk", d_attn, values, preferred_element_type=jnp.float32)
    d_score = (
        weights * (d_prob - jnp.sum(weights * d_prob, axis=-1, keepdims=True)) / math.sqrt(HS)
    ).astype(jnp.bfloat16)
    d_query = jnp.einsum(
        "shqk,skhd->sqhd", d_score, keys_all, preferred_element_type=jnp.float32
    ).astype(jnp.bfloat16)
    d_key = jnp.einsum(
        "shqk,sqhd->skhd", d_score, queries, preferred_element_type=jnp.float32
    ).astype(jnp.bfloat16)
    d_value = jnp.einsum(
        "shqk,sqhd->skhd", rounded, d_attn, preferred_element_type=jnp.float32
    ).astype(jnp.bfloat16)
    d_pack = jnp.stack([d_query, d_key, d_value], axis=2).reshape(rows_all, 3 * local_inner)
    own_rows = D // lax.axis_size("dp")
    piece = shaped
    grad_qkv = lax.psum_scatter(
        lax.dot_general(
            piece, d_pack, (((0,), (0,)), ((), ())), preferred_element_type=jnp.float32
        ),
        "dp",
        scatter_dimension=0,
        tiled=True,
    ).reshape(own_rows, 3, local_inner)
    piece = d_proj
    grad_out = lax.psum_scatter(
        lax.dot_general(
            piece, attended, (((0,), (0,)), ((), ())), preferred_element_type=jnp.float32
        ),
        "dp",
        scatter_dimension=0,
        tiled=True,
    )
    squares = jnp.sum(grad_qkv * grad_qkv) + jnp.sum(grad_out * grad_out)
    squares = lax.psum(squares, ("dp", "mp"))
    rms_value = jnp.sqrt(squares / (4 * D * INNER))
    factor = 1.0 / jnp.maximum(rms_value, 1.0)

    def adam(moment, second, grad):
        normed_grad = grad * factor
        new_moment = BETA_ONE * moment + (1.0 - BETA_ONE) * normed_grad
        new_second = BETA_TWO * second + (1.0 - BETA_TWO) * normed_grad * normed_grad
        return (new_moment, new_second, new_moment / (jnp.sqrt(new_second) + ADAM_EPS))

    mq, vq, uq = adam(moment_qkv, second_qkv, grad_qkv)
    mo, vo, uo = adam(moment_out, second_out, grad_out)
    loss = loss_sum / (samples * lax.axis_size("dp") * LATENT)
    return (mq, vq, uq, mo, vo, uo, loss)


def solution(mesh):
    placed = (
        P("dp", None),
        P("dp", None),
        P("dp"),
        P("dp"),
        P(),
        P(),
        P(),
        P(),
        P(None, None, "mp"),
        P(None, "mp"),
        P(),
        P(),
        P(),
        P("dp", None, "mp"),
        P("dp", "mp"),
        P("dp", None, "mp"),
        P("dp", None, "mp"),
        P("dp", "mp"),
        P("dp", "mp"),
    )
    return jax.shard_map(
        per_device,
        mesh=mesh,
        in_specs=placed,
        out_specs=(
            P("dp", None, "mp"),
            P("dp", None, "mp"),
            P("dp", None, "mp"),
            P("dp", "mp"),
            P("dp", "mp"),
            P("dp", "mp"),
            P(),
        ),
        check_vma=False,
    )
```

profile of v0, /device:TPU:0, one launch (start us, length us, event | category | flops | bytes accessed | tf_op | source)
XLA Modules:
  0.0 635.7 jit_solution(17191373692471560332)
XLA Ops:
  13.0 3.7 fusion.47
  20.4 8.9 %copy.72 = bf16[2048,3,512]{0,2,1:T(8,128)(2,1)} copy(bf16[2048,3,512]{2,0,1:T(8,128)(2,1)} %param.27) | data formatting | bytes 12582912 | tf_op args[8]
  29.3 6.2 convolution_convert_fusion.1
  39.6 2.9 convolution_convert_fusion.6
  42.5 3.0 fusion.141
  52.0 6.2 reduce-scatter.8.cloned.1.call-done
  60.4 3.5 multiply_add_fusion.5
  69.2 5.6 convolution_convert_fusion
  78.9 2.9 convolution_convert_fusion.5
  81.8 3.0 fusion.142
  85.8 3.1 fusion.134
  90.1 76.8 %all-gather.4.cloned.1.call-done = bf16[2048,3,512]{0,2,1:T(8,128)(2,1)} async-done(((bf16[128,3,512]{0,2,1:T(8,128)(2,1)}), bf16[2048,3,512]{0,2,1:T(8,128)(2,1)}) %all-gather.4.cloned.1.call-update) | async-done | bytes 6291472 | tf_op jit(solution)/shard_map/all_gather | solution.py:155
  166.9 5.5 convolution_convert_fusion.2
  178.0 50.2 %all-gather.6.cloned.1.call-done = bf16[2048,512]{1,0:T(8,128)(2,1)} async-done(((bf16[128,512]{1,0:T(8,128)(2,1)}), bf16[2048,512]{1,0:T(8,128)(2,1)}) %all-gather.6.cloned.1.call-update) | async-done | bytes 2097168 | tf_op jit(solution)/shard_map/all_gather | solution.py:156
  228.2 3.6 fusion.140
  244.0 4.9 fusion.80
  251.6 8.8 %all-gather.8.cloned.1.call-done = bf16[256,2048]{1,0:T(8,128)(2,1)} async-done(((bf16[128,2048]{1,0:T(8,128)(2,1)}), bf16[256,2048]{1,0:T(8,128)(2,1)}) %all-gather.8.cloned.1.call-update) | async-done | bytes 1048592 | tf_op jit(solution)/shard_map/all_gather | solution.py:192
  260.5 3.9 fusion.143
  270.9 4.3 fusion.25
  275.3 4.9 fusion.22
  282.4 6.6 %fusion.121 = f32[2048,1536]{1,0:T(8,128)} fusion(bf16[256,1536]{0,1:T(8,128)(2,1)S(1)} %bitcast.271, f32[256,2048]{1,0:T(8,128)S(1)} %get-tuple-element.52, f32[2048]{0:T(1024)S(1)} %bitcast.291, f32[2048]{0:T(1024)S(1)} %bitcast.289, f32[256]{0:T(256)S(1)} %copy-done.27, f32[256]{0:T(256)S(1)} %copy-done.25), kind=kOutput, calls=%fused_computation.187 | convolution fusion | flops 1613234176 | bytes 15484928 | tf_op jit(solution)/shard_map/dot_general | solution.py:213
  291.5 70.3 %reduce-scatter.14.cloned.1.call-done = f32[128,512]{1,0:T(8,128)} async-done(((f32[2048,512]{1,0:T(8,128)}), f32[128,512]{1,0:T(8,128)}) %reduce-scatter.14.cloned.1.call-update) | async-done | bytes 262160 | tf_op jit(solution)/shard_map/reduce_scatter | solution.py:221
  363.4 205.5 %reduce-scatter.12.cloned.1.call-done = f32[128,1536]{1,0:T(8,128)} async-done(((f32[2048,1536]{1,0:T(8,128)}), f32[128,1536]{1,0:T(8,128)}) %reduce-scatter.12.cloned.1.call-update) | async-done | bytes 786448 | tf_op jit(solution)/shard_map/reduce_scatter | solution.py:212
  572.2 40.5 %all-reduce = (f32[]{:T(128)}, f32[]{:T(128)}) all-reduce(f32[]{:T(128)S(6)} %add.239, f32[]{:T(128)} %get-tuple-element.60), channel_id=1, replica_groups=mesh['dp'=16,'mp'=2] {'dp','mp'}, use_global_device_ids=true, to_apply=%region_28.0 | all-reduce | flops 2 | bytes 16 | tf_op jit(solution)/shard_map/psum | solution.py:230
  (167 shorter events, 74.7 us)
Async XLA Ops:
  8.0 34.5 %copy-start = (bf16[2048,512]{1,0:T(8,128)(2,1)S(1)}, bf16[2048,512]{1,0:T(8,128)(2,1)}, u32[]{:S(2)}) copy-start(bf16[2048,512]{1,0:T(8,128)(2,1)} %param.28) | copy-start | bytes 6291460
  8.0 8.7 %copy-start.12 = (f32[16,2048]{1,0:T(8,128)S(1)}, f32[16,2048]{1,0:T(8,128)}, u32[]{:S(2)}) copy-start(f32[16,2048]{1,0:T(8,128)} %param.24) | copy-start | bytes 393220
  8.0 50.1 %reduce-scatter.8.cloned.1.call-start = ((), (), s32[]{:S(2)}) async-start(), calls=%async_computation.8 | async-start | bytes 3145728 | tf_op jit(solution)/shard_map/reduce_scatter | solution.py:140
  8.1 40.5 %copy-start.31 = (f32[17,1]{0,1:T(1,128)}, f32[17,1]{0,1:T(1,128)S(1)}, u32[]{:S(2)}) copy-start(f32[17,1]{0,1:T(1,128)S(1)} %get-tuple-element.62) | copy-start | bytes 208
  8.1 40.5 %copy-start.33 = (f32[17,1]{0,1:T(1,128)}, f32[17,1]{0,1:T(1,128)S(1)}, u32[]{:S(2)}) copy-start(f32[17,1]{0,1:T(1,128)S(1)} %get-tuple-element.63) | copy-start | bytes 208
  45.5 121.4 %all-gather.4.cloned.1.call-start = ((), (), s32[]{:S(2)}) async-start(), calls=%async_computation.5 | async-start | bytes 6684672 | tf_op jit(solution)/shard_map/all_gather | solution.py:155
  47.5 180.7 %all-gather.6.cloned.1.call-start = ((), (), s32[]{:S(2)}) async-start(), calls=%async_computation.6 | async-start | bytes 2228224 | tf_op jit(solution)/shard_map/all_gather | solution.py:156
  48.1 190.8 %reduce-scatter.10.cloned.1.call-start = ((), (), s32[]{:S(2)}) async-start(), calls=%async_computation.9 | async-start | bytes 3145728 | tf_op jit(solution)/shard_map/reduce_scatter | solution.py:140
  48.8 11.5 %copy-start.21 = (f32[128,16]{0,1:T(8,128)}, f32[128,16]{0,1:T(8,128)S(1)}, u32[]{:S(2)}) copy-start(f32[128,16]{0,1:T(8,128)S(1)} %copy.101) | copy-start | bytes 24580
  58.2 7.6 %copy-start.3 = (f32[256,1024]{1,0:T(8,128)S(1)}, f32[256,1024]{1,0:T(8,128)}, u32[]{:S(2)}) copy-start(f32[256,1024]{1,0:T(8,128)} %copy-done.2) | copy-start | bytes 3145732
  84.9 157.3 %reduce-scatter.6.cloned.1.call-start = ((), (), s32[]{:S(2)}) async-start(), calls=%async_computation.7 | async-start | bytes 3145728 | tf_op jit(solution)/shard_map/reduce_scatter | solution.py:140
  88.9 83.5 %copy-start.24 = (f32[256]{0:T(256)}, f32[256]{0:T(256)S(1)}, u32[]{:S(2)}) copy-start(f32[256]{0:T(256)S(1)} %broadcast_multiply_fusion.3) | copy-start | bytes 3076
  89.3 83.1 %copy-start.26 = (f32[256]{0:T(256)}, f32[256]{0:T(256)S(1)}, u32[]{:S(2)}) copy-start(f32[256]{0:T(256)S(1)} %add_rsqrt_fusion.2) | copy-start | bytes 3076
  173.8 4.1 copy-start.7
  231.9 5.8 copy-start.30
  231.9 7.1 %copy-start.23 = (f32[1,1,2048]{2,0,1:T(1,128)S(1)}, f32[1,1,2048]{2,0,1:T(1,128)}, u32[]{:S(2)}) copy-start(f32[1,1,2048]{2,0,1:T(1,128)} %get-tuple-element.37) | copy-start | bytes 24580
  231.9 28.5 %all-gather.8.cloned.1.call-start = ((), (), s32[]{:S(2)}) async-start(), calls=%async_computation.10 | async-start | bytes 1572864 | tf_op jit(solution)/shard_map/all_gather | solution.py:192
  251.6 110.2 %reduce-scatter.14.cloned.1.call-start = ((), (), s32[]{:S(2)}) async-start(), calls=%async_computation.12 | async-start | bytes 4456448 | tf_op jit(solution)/shard_map/reduce_scatter | solution.py:221
  264.4 304.5 %reduce-scatter.12.cloned.1.call-start = ((), (), s32[]{:S(2)}) async-start(), calls=%async_computation.11 | async-start | bytes 13369344 | tf_op jit(solution)/shard_map/reduce_scatter | solution.py:212
  267.9 3.0 copy-start.8
  267.9 3.0 copy-start.36
  618.4 6.6 %copy-start.9 = (f32[128,512]{1,0:T(8,128)S(1)}, f32[128,512]{1,0:T(8,128)}, u32[]{:S(2)}) copy-start(f32[128,512]{1,0:T(8,128)} %reduce-scatter.14.cloned.1.call-done) | copy-start | bytes 786436
  618.5 6.6 %copy-start.15 = (f32[128,512]{1,0:T(8,128)S(1)}, f32[128,512]{1,0:T(8,128)}, u32[]{:S(2)}) copy-start(f32[128,512]{1,0:T(8,128)} %param.37) | copy-start | bytes 786436
  620.8 6.2 copy-start.1
  (21 other events, 32.2 us)
Sparse Core Ops, SparseCore 0:
  45.7 12.4 reduce-scatter.7
  85.0 11.0 reduce-scatter.9
  232.0 8.5 reduce-scatter.5
  251.7 8.6 all-gather.7
Sparse Core Ops, SparseCore 1:
  49.3 117.6 all-gather.3
  169.6 58.6 all-gather.5
  264.5 97.2 reduce-scatter.13
  367.5 201.4 reduce-scatter.11
where the time goes:
time: 645 us; the launch traced here: 636 us
  waiting for transfers between devices  419 us (65%)
  matrix products  88.5 us (14%)
  blocking collectives  42.3 us (7%)
  local copies, waits for them, and re-layouts  34.2 us (5%)
  between operations  26 us (4%)
  other arithmetic  24.9 us (4%)
    reduce_scatter x1, waiting for transfers between devices, per_device(): lax.psum_scatter(lax.dot_general(piece, d_pack, (((0,), (0,)), ((), ())),...  206 us
    all_gather x1, waiting for transfers between devices, per_device(): lax.all_gather(student_qkv, 'dp', axis=0, tiled=True)  76.8 us
    reduce_scatter x1, waiting for transfers between devices, per_device(): lax.psum_scatter(lax.dot_general(piece, attended, (((0,), (0,)), ((), ())...  70.3 us
    all_gather x1, waiting for transfers between devices, per_device(): lax.all_gather(student_out, 'dp', axis=0, tiled=True)  50.2 us
    psum x1, blocking collectives, per_device(): squares = lax.psum(squares, ('dp', 'mp'))  40.5 us
    unnamed x82, local copies, waits for them, and re-layouts  24.4 us
    dot_general x3, matrix products, front(): jnp.dot(shaped, w_qkv.reshape(D, 3 * local_inner), preferred_element_type...  17.3 us
  transfers between devices with their start and end apart: 8, of which 6 were waited for; matrix products, arithmetic and copies ran while one was open for 12% of the time, Pallas kernels for 0%

commit v1 on v0

--- a/solution.py
+++ b/solution.py
@@ -227,7 +227,7 @@
         tiled=True,
     )
     squares = jnp.sum(grad_qkv * grad_qkv) + jnp.sum(grad_out * grad_out)
-    squares = lax.psum(squares, ("dp", "mp"))
+    squares = lax.psum(lax.psum(squares, "mp"), "dp")
     rms_value = jnp.sqrt(squares / (4 * D * INNER))
     factor = 1.0 / jnp.maximum(rms_value, 1.0)
 

time: 645 us -> 689 us (1.068)
  blocking collectives: 42.3 us -> 86.2 us
    psum x1 -> x3, blocking collectives: 40.5 us -> 84.4 us  [the longest x2 43.9 us: per_device(): squares = lax.psum(lax.psum(squares, 'mp'), 'dp')]
  transfers between devices with their start and end apart: 8 -> 8, of which waited for: 6 -> 6; matrix products, arithmetic and copies ran while one was open for 12% -> 11% of each run, Pallas kernels for 0% -> 0%
where the time goes in v1:
time: 689 us; the launch traced here: 680 us
  waiting for transfers between devices  419 us (61%)
  matrix products  88.5 us (13%)
  blocking collectives  86.2 us (13%)
  local copies, waits for them, and re-layouts  34.2 us (5%)
  between operations  25.9 us (4%)
  other arithmetic  24.9 us (4%)
    reduce_scatter x1, waiting for transfers between devices, per_device(): lax.psum_scatter(lax.dot_general(piece, d_pack, (((0,), (0,)), ((), ())),...  206 us
    all_gather x1, waiting for transfers between devices, per_device(): lax.all_gather(student_qkv, 'dp', axis=0, tiled=True)  76.8 us
    reduce_scatter x1, waiting for transfers between devices, per_device(): lax.psum_scatter(lax.dot_general(piece, attended, (((0,), (0,)), ((), ())...  70.3 us
    all_gather x1, waiting for transfers between devices, per_device(): lax.all_gather(student_out, 'dp', axis=0, tiled=True)  50.2 us
    psum x2, blocking collectives, per_device(): squares = lax.psum(lax.psum(squares, 'mp'), 'dp')  43.9 us
    psum x1, blocking collectives, per_device(): loss_sum = lax.psum(loss_part, ('dp', 'mp'))  40.5 us
    unnamed x82, local copies, waits for them, and re-layouts  24.4 us
    dot_general x3, matrix products, front(): jnp.dot(shaped, w_qkv.reshape(D, 3 * local_inner), preferred_element_type...  17.3 us
  transfers between devices with their start and end apart: 8, of which 6 were waited for; matrix products, arithmetic and copies ran while one was open for 11% of the time, Pallas kernels for 0%

profile of v1, /device:TPU:0, one launch (start us, length us, event | category | flops | bytes accessed | tf_op | source)
XLA Modules:
  0.0 679.6 jit_solution(11491431635202387028)
XLA Ops:
  13.0 3.7 fusion.47
  20.4 8.9 %copy.72 = bf16[2048,3,512]{0,2,1:T(8,128)(2,1)} copy(bf16[2048,3,512]{2,0,1:T(8,128)(2,1)} %param.27) | data formatting | bytes 12582912 | tf_op args[8]
  29.3 6.2 convolution_convert_fusion.1
  42.5 3.0 fusion.141
  52.0 6.2 reduce-scatter.8.cloned.1.call-done
  60.4 3.5 multiply_add_fusion.5
  69.2 5.6 convolution_convert_fusion
  81.8 3.0 fusion.142
  85.8 3.1 fusion.134
  90.1 76.8 %all-gather.4.cloned.1.call-done = bf16[2048,3,512]{0,2,1:T(8,128)(2,1)} async-done(((bf16[128,3,512]{0,2,1:T(8,128)(2,1)}), bf16[2048,3,512]{0,2,1:T(8,128)(2,1)}) %all-gather.4.cloned.1.call-update) | async-done | bytes 6291472 | tf_op jit(solution)/shard_map/all_gather | solution.py:155
  166.9 5.5 convolution_convert_fusion.2
  178.0 50.2 %all-gather.6.cloned.1.call-done = bf16[2048,512]{1,0:T(8,128)(2,1)} async-done(((bf16[128,512]{1,0:T(8,128)(2,1)}), bf16[2048,512]{1,0:T(8,128)(2,1)}) %all-gather.6.cloned.1.call-update) | async-done | bytes 2097168 | tf_op jit(solution)/shard_map/all_gather | solution.py:156
  228.2 3.6 fusion.140
  244.0 4.9 fusion.80
  251.6 8.8 %all-gather.8.cloned.1.call-done = bf16[256,2048]{1,0:T(8,128)(2,1)} async-done(((bf16[128,2048]{1,0:T(8,128)(2,1)}), bf16[256,2048]{1,0:T(8,128)(2,1)}) %all-gather.8.cloned.1.call-update) | async-done | bytes 1048592 | tf_op jit(solution)/shard_map/all_gather | solution.py:192
  260.5 3.9 fusion.143
  270.9 4.3 fusion.25
  275.3 4.9 fusion.22
  282.4 6.6 fusion.121
  291.5 70.3 %reduce-scatter.14.cloned.1.call-done = f32[128,512]{1,0:T(8,128)} async-done(((f32[2048,512]{1,0:T(8,128)}), f32[128,512]{1,0:T(8,128)}) %reduce-scatter.14.cloned.1.call-update) | async-done | bytes 262160 | tf_op jit(solution)/shard_map/reduce_scatter | solution.py:221
  363.4 205.5 %reduce-scatter.12.cloned.1.call-done = f32[128,1536]{1,0:T(8,128)} async-done(((f32[2048,1536]{1,0:T(8,128)}), f32[128,1536]{1,0:T(8,128)}) %reduce-scatter.12.cloned.1.call-update) | async-done | bytes 786448 | tf_op jit(solution)/shard_map/reduce_scatter | solution.py:212
  572.2 40.5 %psum.23 = f32[]{:T(128)} all-reduce(f32[]{:T(128)} %get-tuple-element.58), channel_id=1, replica_groups=mesh['dp'=16,'mp'=2] {'dp','mp'}, use_global_device_ids=true, to_apply=%region_31.0 | all-reduce | flops 1 | bytes 8 | tf_op jit(solution)/shard_map/psum | solution.py:193
  612.6 3.0 psum.21
  616.3 41.0 %psum.22 = f32[]{:T(128)} all-reduce(f32[]{:T(128)} %psum.21), channel_id=1, replica_groups=mesh['dp'=16,'mp'=2] {'dp'}, use_global_device_ids=true, to_apply=%region_29.0 | all-reduce | flops 1 | bytes 8 | tf_op jit(solution)/shard_map/psum | solution.py:230
  (169 shorter events, 80.5 us)
Async XLA Ops:
  8.0 34.5 %copy-start = (bf16[2048,512]{1,0:T(8,128)(2,1)S(1)}, bf16[2048,512]{1,0:T(8,128)(2,1)}, u32[]{:S(2)}) copy-start(bf16[2048,512]{1,0:T(8,128)(2,1)} %param.28) | copy-start | bytes 6291460
  8.0 8.7 %copy-start.12 = (f32[16,2048]{1,0:T(8,128)S(1)}, f32[16,2048]{1,0:T(8,128)}, u32[]{:S(2)}) copy-start(f32[16,2048]{1,0:T(8,128)} %param.24) | copy-start | bytes 393220
  8.0 50.1 %reduce-scatter.8.cloned.1.call-start = ((), (), s32[]{:S(2)}) async-start(), calls=%async_computation.8 | async-start | bytes 3145728 | tf_op jit(solution)/shard_map/reduce_scatter | solution.py:140
  8.1 40.5 %copy-start.31 = (f32[17,1]{0,1:T(1,128)}, f32[17,1]{0,1:T(1,128)S(1)}, u32[]{:S(2)}) copy-start(f32[17,1]{0,1:T(1,128)S(1)} %get-tuple-element.60) | copy-start | bytes 208
  8.1 40.5 %copy-start.33 = (f32[17,1]{0,1:T(1,128)}, f32[17,1]{0,1:T(1,128)S(1)}, u32[]{:S(2)}) copy-start(f32[17,1]{0,1:T(1,128)S(1)} %get-tuple-element.61) | copy-start | bytes 208
  45.5 121.4 %all-gather.4.cloned.1.call-start = ((), (), s32[]{:S(2)}) async-start(), calls=%async_computation.5 | async-start | bytes 6684672 | tf_op jit(solution)/shard_map/all_gather | solution.py:155
  47.5 180.7 %all-gather.6.cloned.1.call-start = ((), (), s32[]{:S(2)}) async-start(), calls=%async_computation.6 | async-start | bytes 2228224 | tf_op jit(solution)/shard_map/all_gather | solution.py:156
  48.1 190.8 %reduce-scatter.10.cloned.1.call-start = ((), (), s32[]{:S(2)}) async-start(), calls=%async_computation.9 | async-start | bytes 3145728 | tf_op jit(solution)/shard_map/reduce_scatter | solution.py:140
  48.8 11.5 %copy-start.21 = (f32[128,16]{0,1:T(8,128)}, f32[128,16]{0,1:T(8,128)S(1)}, u32[]{:S(2)}) copy-start(f32[128,16]{0,1:T(8,128)S(1)} %copy.101) | copy-start | bytes 24580
  58.2 7.6 %copy-start.3 = (f32[256,1024]{1,0:T(8,128)S(1)}, f32[256,1024]{1,0:T(8,128)}, u32[]{:S(2)}) copy-start(f32[256,1024]{1,0:T(8,128)} %copy-done.2) | copy-start | bytes 3145732
  84.9 157.3 %reduce-scatter.6.cloned.1.call-start = ((), (), s32[]{:S(2)}) async-start(), calls=%async_computation.7 | async-start | bytes 3145728 | tf_op jit(solution)/shard_map/reduce_scatter | solution.py:140
  88.9 83.5 %copy-start.24 = (f32[256]{0:T(256)}, f32[256]{0:T(256)S(1)}, u32[]{:S(2)}) copy-start(f32[256]{0:T(256)S(1)} %broadcast_multiply_fusion.3) | copy-start | bytes 3076
  89.3 83.1 %copy-start.26 = (f32[256]{0:T(256)}, f32[256]{0:T(256)S(1)}, u32[]{:S(2)}) copy-start(f32[256]{0:T(256)S(1)} %add_rsqrt_fusion.2) | copy-start | bytes 3076
  173.8 4.1 copy-start.7
  231.9 5.8 copy-start.30
  231.9 7.1 %copy-start.23 = (f32[1,1,2048]{2,0,1:T(1,128)S(1)}, f32[1,1,2048]{2,0,1:T(1,128)}, u32[]{:S(2)}) copy-start(f32[1,1,2048]{2,0,1:T(1,128)} %get-tuple-element.35) | copy-start | bytes 24580
  231.9 28.5 %all-gather.8.cloned.1.call-start = ((), (), s32[]{:S(2)}) async-start(), calls=%async_computation.10 | async-start | bytes 1572864 | tf_op jit(solution)/shard_map/all_gather | solution.py:192
  251.6 110.2 %reduce-scatter.14.cloned.1.call-start = ((), (), s32[]{:S(2)}) async-start(), calls=%async_computation.12 | async-start | bytes 4456448 | tf_op jit(solution)/shard_map/reduce_scatter | solution.py:221
  264.4 304.5 %reduce-scatter.12.cloned.1.call-start = ((), (), s32[]{:S(2)}) async-start(), calls=%async_computation.11 | async-start | bytes 13369344 | tf_op jit(solution)/shard_map/reduce_scatter | solution.py:212
  267.9 3.0 copy-start.8
  267.9 3.0 copy-start.36
  663.0 5.9 copy-start.9
  663.0 5.9 copy-start.15
  665.4 5.5 copy-start.1
  (21 other events, 32.2 us)
Sparse Core Ops, SparseCore 0:
  45.7 12.4 reduce-scatter.7
  85.0 11.0 reduce-scatter.9
  232.0 8.5 reduce-scatter.5
  251.7 8.6 all-gather.7
Sparse Core Ops, SparseCore 1:
  49.3 117.6 all-gather.3
  169.6 58.6 all-gather.5
  264.5 97.2 reduce-scatter.13
  367.5 201.4 reduce-scatter.11
